TPU v7x, 128 devices: a whole 4x4x4 slice. The times are simulated.
128 devices in a mesh: expert: 128 (over y, x, z, core).
Axes of the slice: x: 4, y: 4, z: 4, core: 2. Of those that a mesh axis runs over, the one named last changes fastest.
Arguments:
- tokens: bfloat16 [16384, 4096], P('expert'), may hold values from -6 to 6
- norm_gain: float32 [4096], replicated, may hold values from 0.5 to 1.5
- router_weight: bfloat16 [4096, 128], replicated, may hold values from -0.09375 to 0.09375
- expert_ids: int32 [16384, 2], P('expert'), may hold values from 0 to 127, as said below
- gate_proj: bfloat16 [128, 4096, 768], P('expert'), may hold values from -0.09375 to 0.09375
- up_proj: bfloat16 [128, 4096, 768], P('expert'), may hold values from -0.09375 to 0.09375
- down_proj: bfloat16 [128, 768, 4096], P('expert'), may hold values from -0.21875 to 0.21875
- value_weight: bfloat16 [4096], replicated, may hold values from -0.09375 to 0.09375
- value_target: int32 [16384], P('expert'), may hold values from -1 to 1
- recency: float32 [16384], P('expert'), may hold values from 0.25 to 18, as said below
Outputs:
- mixed: bfloat16 [16384, 4096], P('expert')
- values: float32 [16384], P('expert')
- loss: float32 [], replicated
Inputs may be any that keep to these rules, and one draw needn't show every extreme that they name: `expert_ids`: each row names two different experts; among the rows of one device no expert is named more than 3 times. `recency`: positive weights.
All inputs are finite; a program needn't handle non-finite values.
Results may differ from a plain program's by a relative error of at most 0.0055.
Values may be sent and summed in bfloat16 or wider, within the bound.
No kernel may reach another device: no remote copies, remote signals or barrier semaphores. Data moves between devices by JAX's collectives and lax.ppermute only.
A program may use at most 128 MiB of HBM per device.

v0:
```python
import jax
import jax.numpy as jnp
from jax import lax
from jax.sharding import Mesh
from jax.sharding import PartitionSpec as P

EXPERT = ("expert_0", "expert_1", "expert_2", "expert_3")


def by_axis(x, axes):
    for axis in axes:
        x = lax.psum(x, axis)
    return x


def expert_ffn(received, gate_proj, up_proj, down_proj):
    sources, slots, width = received.shape
    flat_input = received.reshape(sources * slots, width)
    gate_part = jnp.dot(flat_input, gate_proj[0], preferred_element_type=jnp.float32)
    up_part = jnp.dot(flat_input, up_proj[0], preferred_element_type=jnp.float32)
    hidden = (jax.nn.silu(gate_part) * up_part).astype(jnp.bfloat16)
    result = jnp.dot(hidden, down_proj[0], preferred_element_type=jnp.float32).astype(jnp.bfloat16)
    return result.reshape(sources, slots, width)


def body(
    tokens,
    norm_gain,
    router_weight,
    expert_ids,
    gate_proj,
    up_proj,
    down_proj,
    value_weight,
    value_target,
    recency,
):
    token_count, width = tokens.shape
    expert_total = router_weight.shape[1]
    capacity = 3 * token_count // expert_total
    wide = tokens.astype(jnp.float32)
    inverse = lax.rsqrt(jnp.mean(wide * wide, axis=1, keepdims=True) + 1e-05)
    normed = (wide * inverse * norm_gain).astype(jnp.bfloat16)
    logits = jnp.dot(normed, router_weight, preferred_element_type=jnp.float32)
    columns = lax.broadcasted_iota(jnp.int32, (1, expert_total), 1)
    first = jnp.sum(jnp.where(expert_ids[:, 0:1] == columns, logits, 0.0), axis=1)
    second = jnp.sum(jnp.where(expert_ids[:, 1:2] == columns, logits, 0.0), axis=1)
    gate_first = jax.nn.sigmoid(first - second)
    gate_second = jax.nn.sigmoid(second - first)
    flat_ids = expert_ids.reshape(-1)
    one_hot = (flat_ids[:, None] == columns).astype(jnp.int32)
    slot_rank = jnp.sum(jnp.cumsum(one_hot, axis=0) * one_hot, axis=1) - 1
    slot_index = flat_ids * capacity + slot_rank
    row_index = jnp.arange(2 * token_count, dtype=jnp.int32) // 2
    source_row = (
        jnp.full((expert_total * capacity,), token_count, dtype=jnp.int32)
        .at[slot_index]
        .set(row_index)
    )
    padded = jnp.concatenate([normed, jnp.zeros((1, width), jnp.bfloat16)], axis=0)
    outgoing = padded[source_row].reshape(expert_total, capacity, width)
    received = lax.all_to_all(outgoing, EXPERT, split_axis=0, concat_axis=0, tiled=True)
    produced = expert_ffn(received, gate_proj, up_proj, down_proj)
    returned = lax.all_to_all(produced, EXPERT, split_axis=0, concat_axis=0, tiled=True)
    flat_back = returned.reshape(expert_total * capacity, width)
    picked = flat_back[slot_index].reshape(token_count, 2, width)
    mixed = (
        wide
        + gate_first[:, None] * picked[:, 0].astype(jnp.float32)
        + gate_second[:, None] * picked[:, 1].astype(jnp.float32)
    ).astype(jnp.bfloat16)
    values = jnp.tanh(jnp.dot(mixed, value_weight, preferred_element_type=jnp.float32))
    error = values - value_target.astype(jnp.float32)
    weighted, weight_total = (
        by_axis(jnp.sum(recency * error * error), EXPERT),
        by_axis(jnp.sum(recency), EXPERT),
    )
    loss = weighted / weight_total
    return (mixed, values, loss)


def solution(mesh):
    finer = Mesh(mesh.devices.reshape(4, 4, 4, 2), ("expert_0", "expert_1", "expert_2", "expert_3"))
    in_specs = (
        P(EXPERT, None),
        P(),
        P(),
        P(EXPERT, None),
        P(EXPERT, None, None),
        P(EXPERT, None, None),
        P(EXPERT, None, None),
        P(),
        P(EXPERT),
        P(EXPERT),
    )
    out_specs = (P(EXPERT, None), P(EXPERT), P())
    return jax.shard_map(body, mesh=finer, in_specs=in_specs, out_specs=out_specs, check_vma=False)
```

profile of v0, /device:TPU:1, one launch (start us, length us, event | category | flops | bytes accessed | tf_op | source)
XLA Modules:
  0.0 242.7 jit_solution(9639308537524238652)
XLA Ops:
  0.6 0.0 copy-start
  0.6 0.0 copy-start.1
  0.7 0.0 copy-start.4
  0.7 0.8 broadcast_multiply_fusion
  1.5 0.8 copy.14
  2.3 0.1 eq.67
  2.4 0.1 eq.63
  2.6 1.5 fusion.9
  4.1 0.1 copy.13
  4.2 0.1 mul.75
  4.4 0.1 copy.16
  4.5 0.2 fusion.24
  4.8 0.2 fusion.25
  5.0 1.4 scatter_custom_fusion
  6.4 0.0 copy-done.1
  6.4 0.0 copy-done.4
  6.4 0.3 fusion.11
  6.8 0.1 concatenate.3
  6.9 4.1 %gather_fusion = bf16[384,4096]{1,0:T(8,128)(2,1)} fusion(bf16[129,4096]{1,0:T(8,128)(2,1)S(1)} %concatenate.3, s32[1024]{0:T(1024)S(1)} %pad_clamp_fusion.1), kind=kCustom, calls=%fused_computation | custom fusion | bytes 6292992 | tf_op jit(solution)/shard_map/gather | solution.py:61
  10.9 7.1 %reshape.104 = bf16[128,3,4096]{2,1,0:T(4,128)(2,1)} reshape(bf16[384,4096]{1,0:T(8,128)(2,1)} %gather_fusion) | data formatting | bytes 6291456 | tf_op jit(solution)/shard_map/reshape | solution.py:61
  18.0 64.2 %all_to_all.10 = bf16[128,3,4096]{2,1,0:T(4,128)(2,1)} all-to-all(bf16[128,3,4096]{2,1,0:T(4,128)(2,1)} %reshape.104), channel_id=1, replica_groups=mesh['expert_0'=4,'expert_1'=4,'expert_2'=4,'expert_3'=2] {'expert_0','e..., dimensions={0} | all-to-all | bytes 6291456 | tf_op jit(solution)/shard_map/all_to_all | solution.py:62
  82.2 7.4 %reshape.105 = bf16[384,4096]{1,0:T(8,128)(2,1)} reshape(bf16[128,3,4096]{2,1,0:T(4,128)(2,1)} %all_to_all.10) | data formatting | bytes 6291456 | tf_op jit(solution)/shard_map/reshape | solution.py:18
  89.6 7.4 %fusion.4 = f32[384,768]{1,0:T(8,128)} fusion(bf16[384,4096]{1,0:T(8,128)(2,1)} %reshape.105, bf16[1,4096,768]{2,1,0:T(8,128)(2,1)} %param.14), kind=kOutput, calls=%fused_computation.7 | convolution fusion | flops 2415919104 | bytes 10616832 | tf_op jit(solution)/shard_map/dot_general | solution.py:19
  97.0 14.2 %fusion.6 = bf16[384,4096]{1,0:T(8,128)(2,1)} fusion(bf16[1,768,4096]{2,1,0:T(8,128)(2,1)} %param.16, bf16[384,4096]{1,0:T(8,128)(2,1)} %reshape.105, bf16[1,4096,768]{2,1,0:T(8,128)(2,1)} %param.15, f32[384,768]{1,0:T(8,128)} %fusion.4), kind=kOutput, calls=%fused_computation.9 | convolution fusion | flops 4835180544 | bytes 20054016 | tf_op jit(solution)/shard_map/dot_general | solution.py:22
  111.2 7.1 %reshape.106 = bf16[128,3,4096]{2,1,0:T(4,128)(2,1)} reshape(bf16[384,4096]{1,0:T(8,128)(2,1)} %fusion.6) | data formatting | bytes 6291456 | tf_op jit(solution)/shard_map/reshape | solution.py:23
  118.3 6.1 %all-to-all-start.1 = ((bf16[128,3,4096]{2,1,0:T(4,128)(2,1)}), bf16[128,3,4096]{2,1,0:T(4,128)(2,1)}, u32[]{:S(2)}, u32[]{:S(2)}) async-start(bf16[128,3,4096]{2,1,0:T(4,128)(2,1)} %reshape.106), calls=%async_computation.1 | async-start | bytes 8388608 | tf_op jit(solution)/shard_map/all_to_all | solution.py:64
  124.4 0.0 copy-done.6
  124.4 0.0 copy-done.5
  124.5 0.0 copy-done
  124.5 0.5 select_reduce_fusion.1
  125.0 51.7 %all-to-all-done.1 = bf16[128,3,4096]{2,1,0:T(4,128)(2,1)} async-done(((bf16[128,3,4096]{2,1,0:T(4,128)(2,1)}), bf16[128,3,4096]{2,1,0:T(4,128)(2,1)}, u32[]{:S(2)}, u32[]{:S(2)}) %all-to-all-start.1) | async-done | bytes 3145760 | tf_op jit(solution)/shard_map/all_to_all | solution.py:64
  176.8 7.4 %reshape.107 = bf16[384,4096]{1,0:T(8,128)(2,1)} reshape(bf16[128,3,4096]{2,1,0:T(4,128)(2,1)} %all-to-all-done.1) | data formatting | bytes 6291456 | tf_op jit(solution)/shard_map/reshape | solution.py:65
  184.2 7.5 %gather_fusion.1 = bf16[256,4096]{1,0:T(8,128)(2,1)} fusion(bf16[384,4096]{1,0:T(8,128)(2,1)} %reshape.107, s32[1024]{0:T(1024)S(1)} %pad_clamp_fusion), kind=kCustom, calls=%fused_computation.1 | custom fusion | bytes 4195328 | tf_op jit(solution)/shard_map/gather | solution.py:66
  191.7 3.2 %reshape.108 = bf16[128,2,4096]{2,1,0:T(2,128)(2,1)S(1)} reshape(bf16[256,4096]{1,0:T(8,128)(2,1)} %gather_fusion.1) | data formatting | bytes 4194304 | tf_op jit(solution)/shard_map/reshape | solution.py:66
  194.9 0.0 copy-start.2
  194.9 4.7 %fusion.33 = (bf16[128,1,4096]{2,1,0:T(2,128)(2,1)S(1)}, bf16[128,1,4096]{2,1,0:T(2,128)(2,1)S(1)}) fusion(bf16[128,2,4096]{2,1,0:T(2,128)(2,1)S(1)} %reshape.108), kind=kLoop, calls=%fused_computation.61 | loop fusion | bytes 4194304 | tf_op jit(solution)/shard_map/slice | solution.py:69
  199.6 0.0 copy-done.2
  199.6 0.0 copy-start.7
  199.6 0.0 copy-start.8
  199.6 4.2 %fusion.13 = bf16[128,4096]{1,0:T(8,128)(2,1)S(1)} fusion(bf16[128,4096]{1,0:T(8,128)(2,1)S(1)} %copy-done.2, bf16[128,1,4096]{2,1,0:T(2,128)(2,1)S(1)} %get-tuple-element.16, bf16[128,1,4096]{2,1,0:T(2,128)(2,1)S(1)} %get-tuple-element.15, f32[128]{0:T(128)S(1)} %get-tuple-element.18, f32[128]{0:T(128)S(1)} %get-tuple-element.17), kind=kLoop, calls=%fused_computation.17 | loop fusion | flops 4194304 | bytes 4195328 | tf_op jit(solution)/shard_map/convert_element_type | solution.py:71
  203.8 0.0 copy-done.7
  203.8 0.0 copy-start.3
  203.8 1.5 fusion.32
  205.3 7.5 %all-reduce.3 = (f32[]{:T(128)}, f32[]{:T(128)}) all-reduce(f32[]{:T(128)} %get-tuple-element.6, f32[]{:T(128)} %get-tuple-element.5), channel_id=1, replica_groups=mesh['expert_0'=4,'expert_1'=4,'expert_2'=4,'expert_3'=2] {'expert_0'}, use_global_device_ids=true, to_apply=%region_8.9 | all-reduce | flops 2 | bytes 16 | tf_op jit(solution)/shard_map/psum | solution.py:12
  212.8 7.5 %all-reduce.2 = (f32[]{:T(128)}, f32[]{:T(128)}) all-reduce(f32[]{:T(128)} %get-tuple-element.11, f32[]{:T(128)} %get-tuple-element.12), channel_id=1, replica_groups=mesh['expert_0'=4,'expert_1'=4,'expert_2'=4,'expert_3'=2] {'expert_1'}, use_global_device_ids=true, to_apply=%region_9.10 | all-reduce | flops 2 | bytes 16 | tf_op jit(solution)/shard_map/psum | solution.py:12
  220.3 8.0 %all-reduce.1 = (f32[]{:T(128)}, f32[]{:T(128)}) all-reduce(f32[]{:T(128)} %get-tuple-element.9, f32[]{:T(128)} %get-tuple-element.10), channel_id=1, replica_groups=mesh['expert_0'=4,'expert_1'=4,'expert_2'=4,'expert_3'=2] {'expert_2'}, use_global_device_ids=true, to_apply=%region_10.11 | all-reduce | flops 2 | bytes 16 | tf_op jit(solution)/shard_map/psum | solution.py:12
  228.3 12.0 %all-reduce.4 = (f32[]{:T(128)}, f32[]{:T(128)}) all-reduce(f32[]{:T(128)} %get-tuple-element.7, f32[]{:T(128)} %get-tuple-element.8), channel_id=1, replica_groups=mesh['expert_0'=4,'expert_1'=4,'expert_2'=4,'expert_3'=2] {'expert_3'}, use_global_device_ids=true, to_apply=%region_11.12 | all-reduce | flops 2 | bytes 16 | tf_op jit(solution)/shard_map/psum | solution.py:12
  241.5 0.0 copy-done.3
  (19 shorter events, 0.1 us)
Async XLA Ops:
  0.6 123.8 %copy-start = (bf16[4096,128]{1,0:T(8,128)(2,1)S(1)}, bf16[4096,128]{1,0:T(8,128)(2,1)}, u32[]{:S(2)}) copy-start(bf16[4096,128]{1,0:T(8,128)(2,1)} %param.12) | copy-start | bytes 3145732
  0.6 5.8 %copy-start.1 = (bf16[128,4096]{1,0:T(8,128)(2,1)S(1)}, bf16[128,4096]{1,0:T(8,128)(2,1)}, u32[]{:S(2)}) copy-start(bf16[128,4096]{1,0:T(8,128)(2,1)} %param.10) | copy-start | bytes 3145732
  0.7 5.8 %copy-start.4 = (f32[4096]{0:T(1024)S(1)}, f32[4096]{0:T(1024)}, u32[]{:S(2)}) copy-start(f32[4096]{0:T(1024)} %param.11) | copy-start | bytes 49156
  118.3 6.1 %copy-start.6 = (bf16[4096]{0:T(1024)(128)(2,1)S(1)}, bf16[4096]{0:T(1024)(128)(2,1)}, u32[]{:S(2)}) copy-start(bf16[4096]{0:T(1024)(128)(2,1)} %param.17) | copy-start | bytes 24580
  118.3 6.2 %copy-start.5 = (s32[128,2]{0,1:T(2,128)S(1)}, s32[128,2]{0,1:T(2,128)}, u32[]{:S(2)}) copy-start(s32[128,2]{0,1:T(2,128)} %param.13) | copy-start | bytes 3076
  118.3 58.5 %all-to-all-start.1 = ((bf16[128,3,4096]{2,1,0:T(4,128)(2,1)}), bf16[128,3,4096]{2,1,0:T(4,128)(2,1)}, u32[]{:S(2)}, u32[]{:S(2)}) async-start(bf16[128,3,4096]{2,1,0:T(4,128)(2,1)} %reshape.106), calls=%async_computation.1 | async-start | bytes 8388608 | tf_op jit(solution)/shard_map/all_to_all | solution.py:64
  194.9 4.7 %copy-start.2 = (bf16[128,4096]{1,0:T(8,128)(2,1)S(1)}, bf16[128,4096]{1,0:T(8,128)(2,1)}, u32[]{:S(2)}) copy-start(bf16[128,4096]{1,0:T(8,128)(2,1)} %param.10) | copy-start | bytes 3145732
  199.6 4.2 %copy-start.7 = (f32[128]{0:T(128)S(1)}, f32[128]{0:T(128)}, u32[]{:S(2)}) copy-start(f32[128]{0:T(128)} %param.19) | copy-start | bytes 1540
  199.6 4.2 %copy-start.8 = (s32[128]{0:T(128)S(1)}, s32[128]{0:T(128)}, u32[]{:S(2)}) copy-start(s32[128]{0:T(128)} %param.18) | copy-start | bytes 1540
  203.8 37.7 %copy-start.3 = (bf16[128,4096]{1,0:T(8,128)(2,1)}, bf16[128,4096]{1,0:T(8,128)(2,1)S(1)}, u32[]{:S(2)}) copy-start(bf16[128,4096]{1,0:T(8,128)(2,1)S(1)} %fusion.13) | copy-start | bytes 3145732
where the time goes:
time: 244 us; the launch traced here: 243 us
  blocking collectives  99.1 us (41%)
  waiting for transfers between devices  51.7 us (21%)
  local copies, waits for them, and re-layouts  51.4 us (21%)
  matrix products  23.6 us (10%)
  other arithmetic  7.35 us (3%)
  starting transfers between devices  6.1 us (2%)
  between operations  3.29 us (1%)
    all_to_all x1, blocking collectives, body(): lax.all_to_all(outgoing, EXPERT, split_axis=0, concat_axis=0, tiled=True)  64.2 us
    all_to_all x1, waiting for transfers between devices, body(): lax.all_to_all(produced, EXPERT, split_axis=0, concat_axis=0, tiled=True)  51.7 us
    psum x4, blocking collectives, by_axis(): x = lax.psum(x, axis)  34.9 us
    dot_general x1, matrix products, expert_ffn(): jnp.dot(hidden, down_proj[0], preferred_element_type=jnp.float32)  14.2 us
    gather x1, local copies, waits for them, and re-layouts, body(): picked = flat_back[slot_index].reshape(token_count, 2, width)  7.53 us
    reshape x1, local copies, waits for them, and re-layouts, body(): flat_back = returned.reshape(expert_total * capacity, width)  7.42 us
    reshape x1, local copies, waits for them, and re-layouts, expert_ffn(): flat_input = received.reshape(sources * slots, width)  7.4 us
    dot_general x1, matrix products, expert_ffn(): jnp.dot(flat_input, gate_proj[0], preferred_element_type=jnp.float32)  7.38 us
  transfers between devices with their start and end apart: 1, of which 1 were waited for; matrix products, arithmetic and copies ran while one was open for 0% of the time, Pallas kernels for 0%

commit v1 on v0

--- a/solution.py
+++ b/solution.py
@@ -9,7 +9,7 @@
 
 def by_axis(x, axes):
     for axis in axes:
-        x = lax.psum(x, axis)
+        x = jnp.sum(lax.all_gather(x, axis), axis=0)
     return x
 
 

time: 244 us -> 260 us (1.066)
  local copies, waits for them, and re-layouts: 51.4 us -> 65.1 us
  other arithmetic: 7.35 us -> 12.2 us
  blocking collectives: 99.1 us -> 96.4 us
    psum x4 -> x0, blocking collectives: 34.9 us -> none  [by_axis(): x = lax.psum(x, axis)]
    unnamed x0 -> x4, blocking collectives: none -> 32.2 us
    unnamed x21 -> x49, local copies, waits for them, and re-layouts: 0.85 us -> 14.5 us
    reduce_sum x0 -> x8, other arithmetic: none -> 4.87 us  [by_axis(): x = jnp.sum(lax.all_gather(x, axis), axis=0)]
where the time goes in v1:
time: 260 us; the launch traced here: 258 us
  blocking collectives  96.4 us (37%)
  local copies, waits for them, and re-layouts  65.1 us (25%)
  waiting for transfers between devices  51.2 us (20%)
  matrix products  23.8 us (9%)
  other arithmetic  12.2 us (5%)
  starting transfers between devices  6.11 us (2%)
  between operations  3.47 us (1%)
    all_to_all x1, blocking collectives, body(): lax.all_to_all(outgoing, EXPERT, split_axis=0, concat_axis=0, tiled=True)  64.2 us
    all_to_all x1, waiting for transfers between devices, body(): lax.all_to_all(produced, EXPERT, split_axis=0, concat_axis=0, tiled=True)  51.2 us
    unnamed x4, blocking collectives  32.2 us
    unnamed x49, local copies, waits for them, and re-layouts  14.5 us
    dot_general x1, matrix products, expert_ffn(): jnp.dot(hidden, down_proj[0], preferred_element_type=jnp.float32)  14.3 us
    gather x1, local copies, waits for them, and re-layouts, body(): picked = flat_back[slot_index].reshape(token_count, 2, width)  7.53 us
    reshape x1, local copies, waits for them, and re-layouts, body(): flat_back = returned.reshape(expert_total * capacity, width)  7.42 us
    reshape x1, local copies, waits for them, and re-layouts, expert_ffn(): flat_input = received.reshape(sources * slots, width)  7.4 us
  transfers between devices with their start and end apart: 1, of which 1 were waited for; matrix products, arithmetic and copies ran while one was open for 0% of the time, Pallas kernels for 0%

profile of v1, /device:TPU:1, one launch (start us, length us, event | category | flops | bytes accessed | tf_op | source)
XLA Modules:
  0.0 258.2 jit_solution(8719359447380530503)
XLA Ops:
  0.7 0.8 broadcast_multiply_fusion
  1.5 0.8 copy.14
  2.6 1.5 fusion.9
  4.2 0.1 mul.75
  4.5 0.2 fusion.24
  4.8 0.2 fusion.25
  5.0 1.4 scatter_custom_fusion
  6.4 0.3 fusion.11
  6.9 4.1 %gather_fusion = bf16[384,4096]{1,0:T(8,128)(2,1)} fusion(bf16[129,4096]{1,0:T(8,128)(2,1)S(1)} %concatenate.3, s32[1024]{0:T(1024)S(1)} %pad_clamp_fusion.1), kind=kCustom, calls=%fused_computation | custom fusion | bytes 6292992 | tf_op jit(solution)/shard_map/gather | solution.py:61
  10.9 7.1 %reshape.104 = bf16[128,3,4096]{2,1,0:T(4,128)(2,1)} reshape(bf16[384,4096]{1,0:T(8,128)(2,1)} %gather_fusion) | data formatting | bytes 6291456 | tf_op jit(solution)/shard_map/reshape | solution.py:61
  18.0 64.2 %all_to_all.10 = bf16[128,3,4096]{2,1,0:T(4,128)(2,1)} all-to-all(bf16[128,3,4096]{2,1,0:T(4,128)(2,1)} %reshape.104), channel_id=1, replica_groups=mesh['expert_0'=4,'expert_1'=4,'expert_2'=4,'expert_3'=2] {'expert_0','e..., dimensions={0} | all-to-all | bytes 6291456 | tf_op jit(solution)/shard_map/all_to_all | solution.py:62
  82.2 7.4 %reshape.105 = bf16[384,4096]{1,0:T(8,128)(2,1)} reshape(bf16[128,3,4096]{2,1,0:T(4,128)(2,1)} %all_to_all.10) | data formatting | bytes 6291456 | tf_op jit(solution)/shard_map/reshape | solution.py:18
  89.6 7.4 %fusion.4 = f32[384,768]{1,0:T(8,128)} fusion(bf16[384,4096]{1,0:T(8,128)(2,1)} %reshape.105, bf16[1,4096,768]{2,1,0:T(8,128)(2,1)} %param.14), kind=kOutput, calls=%fused_computation.7 | convolution fusion | flops 2415919104 | bytes 10616832 | tf_op jit(solution)/shard_map/dot_general | solution.py:19
  97.0 14.3 %fusion.6 = bf16[384,4096]{1,0:T(8,128)(2,1)} fusion(bf16[1,768,4096]{2,1,0:T(8,128)(2,1)} %param.16, bf16[384,4096]{1,0:T(8,128)(2,1)} %reshape.105, bf16[1,4096,768]{2,1,0:T(8,128)(2,1)} %param.15, f32[384,768]{1,0:T(8,128)} %fusion.4), kind=kOutput, calls=%fused_computation.9 | convolution fusion | flops 4835180544 | bytes 20054016 | tf_op jit(solution)/shard_map/dot_general | solution.py:22
  111.2 7.1 %reshape.106 = bf16[128,3,4096]{2,1,0:T(4,128)(2,1)} reshape(bf16[384,4096]{1,0:T(8,128)(2,1)} %fusion.6) | data formatting | bytes 6291456 | tf_op jit(solution)/shard_map/reshape | solution.py:23
  118.3 6.1 %all-to-all-start.1 = ((bf16[128,3,4096]{2,1,0:T(4,128)(2,1)}), bf16[128,3,4096]{2,1,0:T(4,128)(2,1)}, u32[]{:S(2)}, u32[]{:S(2)}) async-start(bf16[128,3,4096]{2,1,0:T(4,128)(2,1)} %reshape.106), calls=%async_computation.1 | async-start | bytes 8388608 | tf_op jit(solution)/shard_map/all_to_all | solution.py:64
  124.5 0.6 dynamic-slice
  125.1 0.5 select_reduce_fusion.1
  125.6 51.2 %all-to-all-done.1 = bf16[128,3,4096]{2,1,0:T(4,128)(2,1)} async-done(((bf16[128,3,4096]{2,1,0:T(4,128)(2,1)}), bf16[128,3,4096]{2,1,0:T(4,128)(2,1)}, u32[]{:S(2)}, u32[]{:S(2)}) %all-to-all-start.1) | async-done | bytes 3145760 | tf_op jit(solution)/shard_map/all_to_all | solution.py:64
  176.8 7.4 %reshape.107 = bf16[384,4096]{1,0:T(8,128)(2,1)} reshape(bf16[128,3,4096]{2,1,0:T(4,128)(2,1)} %all-to-all-done.1) | data formatting | bytes 6291456 | tf_op jit(solution)/shard_map/reshape | solution.py:65
  184.2 7.5 %gather_fusion.1 = bf16[256,4096]{1,0:T(8,128)(2,1)} fusion(bf16[384,4096]{1,0:T(8,128)(2,1)} %reshape.107, s32[1024]{0:T(1024)S(1)} %pad_clamp_fusion), kind=kCustom, calls=%fused_computation.1 | custom fusion | bytes 4195328 | tf_op jit(solution)/shard_map/gather | solution.py:66
  191.7 3.2 %reshape.108 = bf16[128,2,4096]{2,1,0:T(2,128)(2,1)S(1)} reshape(bf16[256,4096]{1,0:T(8,128)(2,1)} %gather_fusion.1) | data formatting | bytes 4194304 | tf_op jit(solution)/shard_map/reshape | solution.py:66
  194.9 4.7 %fusion.33 = (bf16[128,1,4096]{2,1,0:T(2,128)(2,1)S(1)}, bf16[128,1,4096]{2,1,0:T(2,128)(2,1)S(1)}) fusion(bf16[128,2,4096]{2,1,0:T(2,128)(2,1)S(1)} %reshape.108), kind=kLoop, calls=%fused_computation.61 | loop fusion | bytes 4194304 | tf_op jit(solution)/shard_map/slice | solution.py:69
  199.7 4.2 %fusion.13 = bf16[128,4096]{1,0:T(8,128)(2,1)S(1)} fusion(bf16[128,4096]{1,0:T(8,128)(2,1)S(1)} %copy-done.2, bf16[128,1,4096]{2,1,0:T(2,128)(2,1)S(1)} %get-tuple-element.16, bf16[128,1,4096]{2,1,0:T(2,128)(2,1)S(1)} %get-tuple-element.15, f32[128]{0:T(128)S(1)} %get-tuple-element.18, f32[128]{0:T(128)S(1)} %get-tuple-element.17), kind=kLoop, calls=%fused_computation.17 | loop fusion | flops 4194304 | bytes 4195328 | tf_op jit(solution)/shard_map/convert_element_type | solution.py:71
  203.9 1.6 fusion.32
  205.5 1.3 dynamic-update-slice.4
  206.8 1.4 dynamic-update-slice
  208.2 0.7 dynamic-slice.1
  208.8 6.8 %all-reduce.11 = (f32[4]{0:T(128)S(1)}, f32[4]{0:T(128)S(1)}) all-reduce(f32[4]{0:T(128)S(1)} %dynamic-update-slice, f32[4]{0:T(128)S(1)} %dynamic-update-slice.4), channel_id=1, replica_groups=mesh['expert_0'=4,'expert_1'=4,'expert_2'=4,'expert_3'=2] {'expert_0'}, use_global_device_ids=true, to_apply=%add.1 | all-reduce | flops 8 | bytes 64
  215.6 0.6 reduce_sum.136
  216.2 0.6 reduce_sum.131
  216.8 1.4 dynamic-update-slice.5
  218.2 1.4 dynamic-update-slice.1
  219.6 0.7 dynamic-slice.2
  220.3 6.9 %all-reduce.10 = (f32[4]{0:T(128)S(1)}, f32[4]{0:T(128)S(1)}) all-reduce(f32[4]{0:T(128)S(1)} %dynamic-update-slice.1, f32[4]{0:T(128)S(1)} %dynamic-update-slice.5), channel_id=1, replica_groups=mesh['expert_0'=4,'expert_1'=4,'expert_2'=4,'expert_3'=2] {'expert_1'}, use_global_device_ids=true, to_apply=%add.2 | all-reduce | flops 8 | bytes 64
  227.2 0.6 reduce_sum.137
  227.8 0.6 reduce_sum.132
  228.4 1.4 dynamic-update-slice.6
  229.7 1.4 dynamic-update-slice.2
  231.2 0.7 dynamic-slice.3
  231.9 7.2 %all-reduce.9 = (f32[4]{0:T(128)S(1)}, f32[4]{0:T(128)S(1)}) all-reduce(f32[4]{0:T(128)S(1)} %dynamic-update-slice.2, f32[4]{0:T(128)S(1)} %dynamic-update-slice.6), channel_id=1, replica_groups=mesh['expert_0'=4,'expert_1'=4,'expert_2'=4,'expert_3'=2] {'expert_2'}, use_global_device_ids=true, to_apply=%add.3 | all-reduce | flops 8 | bytes 64
  239.1 0.6 reduce_sum.138
  239.7 0.6 reduce_sum.133
  240.3 1.4 dynamic-update-slice.7
  241.6 1.4 dynamic-update-slice.3
  243.1 11.3 %all-reduce.12 = (f32[2]{0:T(128)S(1)}, f32[2]{0:T(128)S(1)}) all-reduce(f32[2]{0:T(128)S(1)} %dynamic-update-slice.3, f32[2]{0:T(128)S(1)} %dynamic-update-slice.7), channel_id=1, replica_groups=mesh['expert_0'=4,'expert_1'=4,'expert_2'=4,'expert_3'=2] {'expert_3'}, use_global_device_ids=true, to_apply=%add.4 | all-reduce | flops 4 | bytes 32
  254.4 0.7 reduce_sum.139
  255.1 0.6 reduce_sum.134
  (55 shorter events, 0.8 us)
Async XLA Ops:
  0.6 124.4 %copy-start = (bf16[4096,128]{1,0:T(8,128)(2,1)S(1)}, bf16[4096,128]{1,0:T(8,128)(2,1)}, u32[]{:S(2)}) copy-start(bf16[4096,128]{1,0:T(8,128)(2,1)} %param.12) | copy-start | bytes 3145732
  0.6 5.8 %copy-start.1 = (bf16[128,4096]{1,0:T(8,128)(2,1)S(1)}, bf16[128,4096]{1,0:T(8,128)(2,1)}, u32[]{:S(2)}) copy-start(bf16[128,4096]{1,0:T(8,128)(2,1)} %param.10) | copy-start | bytes 3145732
  0.7 5.8 %copy-start.4 = (f32[4096]{0:T(1024)S(1)}, f32[4096]{0:T(1024)}, u32[]{:S(2)}) copy-start(f32[4096]{0:T(1024)} %param.11) | copy-start | bytes 49156
  118.3 6.1 %copy-start.6 = (bf16[4096]{0:T(1024)(128)(2,1)S(1)}, bf16[4096]{0:T(1024)(128)(2,1)}, u32[]{:S(2)}) copy-start(bf16[4096]{0:T(1024)(128)(2,1)} %param.17) | copy-start | bytes 24580
  118.3 6.2 %copy-start.12 = (u32[128]{0:T(128)S(1)}, u32[128]{0:T(128)}, u32[]{:S(2)}) copy-start(u32[128]{0:T(128)} %constant.53) | copy-start | bytes 1540
  118.3 6.7 %copy-start.5 = (s32[128,2]{0,1:T(2,128)S(1)}, s32[128,2]{0,1:T(2,128)}, u32[]{:S(2)}) copy-start(s32[128,2]{0,1:T(2,128)} %param.13) | copy-start | bytes 3076
  118.3 58.5 %all-to-all-start.1 = ((bf16[128,3,4096]{2,1,0:T(4,128)(2,1)}), bf16[128,3,4096]{2,1,0:T(4,128)(2,1)}, u32[]{:S(2)}, u32[]{:S(2)}) async-start(bf16[128,3,4096]{2,1,0:T(4,128)(2,1)} %reshape.106), calls=%async_computation.1 | async-start | bytes 8388608 | tf_op jit(solution)/shard_map/all_to_all | solution.py:64
  194.9 4.7 %copy-start.2 = (bf16[128,4096]{1,0:T(8,128)(2,1)S(1)}, bf16[128,4096]{1,0:T(8,128)(2,1)}, u32[]{:S(2)}) copy-start(bf16[128,4096]{1,0:T(8,128)(2,1)} %param.10) | copy-start | bytes 3145732
  199.6 4.3 %copy-start.7 = (f32[128]{0:T(128)S(1)}, f32[128]{0:T(128)}, u32[]{:S(2)}) copy-start(f32[128]{0:T(128)} %param.19) | copy-start | bytes 1540
  199.6 4.3 %copy-start.8 = (s32[128]{0:T(128)S(1)}, s32[128]{0:T(128)}, u32[]{:S(2)}) copy-start(s32[128]{0:T(128)} %param.18) | copy-start | bytes 1540
  199.6 8.5 %copy-start.11 = (u32[128]{0:T(128)S(1)}, u32[128]{0:T(128)}, u32[]{:S(2)}) copy-start(u32[128]{0:T(128)} %constant.58) | copy-start | bytes 1540
  199.7 20.0 %copy-start.10 = (u32[128]{0:T(128)S(1)}, u32[128]{0:T(128)}, u32[]{:S(2)}) copy-start(u32[128]{0:T(128)} %constant.63) | copy-start | bytes 1540
  199.7 31.5 %copy-start.9 = (u32[128]{0:T(128)S(1)}, u32[128]{0:T(128)}, u32[]{:S(2)}) copy-start(u32[128]{0:T(128)} %constant.68) | copy-start | bytes 1540
  203.9 53.2 %copy-start.3 = (bf16[128,4096]{1,0:T(8,128)(2,1)}, bf16[128,4096]{1,0:T(8,128)(2,1)S(1)}, u32[]{:S(2)}) copy-start(bf16[128,4096]{1,0:T(8,128)(2,1)S(1)} %fusion.13) | copy-start | bytes 3145732
